TPU v7x, 512 devices: a whole 4x8x8 slice. The times are simulated.
512 devices in a mesh: row: 16 (over x, y_lo, core), col: 32 (over z, y_hi).
Axes of the slice: x: 4, y: 8 (y_hi: 4, y_lo: 2; y = y_hi * 2 + y_lo), z: 8, core: 2. Of those that a mesh axis runs over, the one named last changes fastest.
Arguments:
- item_ids: int32 [131072], P(('row', 'col')), may hold values from 0 to 1023
- user_lengths: int32 [32], replicated, may hold values from 1 to 8192, 131072 in all
- catalogue: bfloat16 [1024, 1024], P(('row', 'col')), may hold values from -6 to 6
- tap_lengths: int32 [1, 1024], replicated, may hold values from 64 to 256
- conv_taps: bfloat16 [1, 256, 1024], replicated, may hold values from -0.375 to 0.375
- norm_gains: float32 [1, 2, 1024], replicated, may hold values from 0.1 to 1.9
- gate_weight: bfloat16 [1, 1024, 1024], P(None, 'col'), may hold values from -0.1875 to 0.1875
- up_weight: bfloat16 [1, 1024, 1024], P(None, 'col'), may hold values from -0.1875 to 0.1875
- down_weight: bfloat16 [1, 1024, 1024], P(None, 'col'), may hold values from -0.1875 to 0.1875
Outputs:
- history_out: bfloat16 [131072, 1024], P(('row', 'col'))
Inputs may be any that keep to these rules, and one draw needn't show every extreme that they name: `user_lengths`: the 32 lengths sum to 131072.
All inputs are finite; a program needn't handle non-finite values.
Results may differ from a plain program's by a relative error of at most 0.0054.
Values may be sent and summed in bfloat16 or wider, within the bound.
A program may use at most 64 MiB of HBM per device.

v0:
```python
import jax
import jax.numpy as jnp
from jax import lax
from jax.sharding import Mesh
from jax.sharding import PartitionSpec as P

ROW_COL = ("row", "col_0", "col_1")
COL = ("col_0", "col_1")


epsilon = 1e-06
group_taps = 32


def from_behind(block, axis, distance):
    devices = range(lax.axis_size(axis))
    route = [(i - distance, i) for i in devices if i - distance in devices]
    return lax.ppermute(block, axis, route)


def in_one_piece(arrays, axis, dim, along):
    both = jnp.concatenate(arrays, axis=along)
    result, at, outs = (lax.all_gather(both, axis, axis=dim, tiled=True), 0, [])
    for a in arrays:
        outs.append(lax.slice_in_dim(result, at, at + a.shape[along], axis=along))
        at += a.shape[along]
    return tuple(outs)


def whole_of(array, axes, dim):
    result = array
    for number in range(len(axes) - 1, -1, -1):
        result = lax.all_gather(result, axes[number], axis=dim, tiled=True)
    return result


def rms_norm(values, gains):
    scale = lax.rsqrt(jnp.mean(values * values, axis=-1, keepdims=True) + epsilon)
    return values * scale * gains


def token_ages(positions, user_starts):
    reached = user_starts[None, :] <= positions[:, None]
    fallback = jnp.minimum(positions, 0)[:, None]
    seg_start = jnp.max(jnp.where(reached, user_starts[None, :], fallback), axis=1)
    return positions - seg_start


def earlier_items(item_ids, wanted):
    current = item_ids
    pieces = []
    current = from_behind(current, ROW_COL, 1)
    pieces = [current] + pieces
    return pieces[0][-wanted:]


def convolve(extended, tap_table, token_age, out_rows):
    reach = extended.shape[0] - out_rows
    groups = -(-tap_table.shape[0] // group_taps)

    def one_group(group_index, accumulated):
        for within in range(group_taps):
            lag_index = group_index * group_taps + within
            shifted = lax.dynamic_slice_in_dim(extended, reach - lag_index, out_rows, 0)
            weights = lax.dynamic_slice_in_dim(tap_table, lag_index, 1, 0)
            keep = (lag_index <= token_age)[:, None]
            accumulated = accumulated + jnp.where(keep, shifted * weights, 0.0)
        return accumulated

    blank = jnp.zeros((out_rows, extended.shape[1]), jnp.float32)
    return lax.fori_loop(0, groups, one_group, blank)


def feed_forward(hidden, gains_row, gate_rows, up_rows, down_rows):
    inner = rms_norm(hidden, gains_row).astype(jnp.bfloat16)
    shards = in_one_piece((gate_rows, up_rows), COL, 0, 1)
    columns = inner
    first_sum = jnp.dot(columns, shards[0], preferred_element_type=jnp.float32)
    second_sum = jnp.dot(columns, shards[1], preferred_element_type=jnp.float32)
    activated = (jax.nn.silu(first_sum) * second_sum).astype(jnp.bfloat16)
    columns = activated
    projected = jnp.dot(columns, whole_of(down_rows, COL, 0), preferred_element_type=jnp.float32)
    return hidden + projected


def body(
    item_ids,
    user_lengths,
    catalogue,
    tap_lengths,
    conv_taps,
    norm_gains,
    gate_weight,
    up_weight,
    down_weight,
):
    row_count = item_ids.shape[0]
    reach = conv_taps.shape[1] - 1
    layer_count = conv_taps.shape[0]
    catalogue_all = lax.all_gather(catalogue, ROW_COL, axis=0, tiled=True)
    device_index = lax.axis_index("row") * lax.axis_size(COL) + lax.axis_index(COL)
    first_row = device_index * row_count
    user_starts = jnp.cumsum(user_lengths) - user_lengths
    lag_column = jnp.arange(conv_taps.shape[1], dtype=jnp.int32)[:, None]
    tap_tables = conv_taps.astype(jnp.float32) * (
        lag_column[None] < tap_lengths[:, None, :]
    ).astype(jnp.float32)
    extra = reach * layer_count
    wide_ids = jnp.concatenate([earlier_items(item_ids, extra), item_ids], axis=0)
    hidden = jnp.take(catalogue_all, wide_ids, axis=0).astype(jnp.float32)
    positions = first_row - extra + jnp.arange(row_count + extra, dtype=jnp.int32)
    all_ages = token_ages(positions, user_starts)
    out_rows = row_count + reach * (layer_count - 1)
    normed = rms_norm(hidden, norm_gains[0, 0]).astype(jnp.bfloat16)
    hidden = hidden[-out_rows:] + convolve(normed, tap_tables[0], all_ages[-out_rows:], out_rows)
    hidden = feed_forward(hidden, norm_gains[0, 1], gate_weight[0], up_weight[0], down_weight[0])
    return hidden.astype(jnp.bfloat16)


def solution(mesh):
    finer = Mesh(mesh.devices.reshape(mesh.shape["row"], 8, 4), ("row", "col_0", "col_1"))
    placed = (
        P(ROW_COL),
        P(),
        P(ROW_COL, None),
        P(),
        P(),
        P(),
        P(None, COL, None),
        P(None, COL, None),
        P(None, COL, None),
    )
    return jax.shard_map(
        body, mesh=finer, in_specs=placed, out_specs=P(ROW_COL, None), check_vma=False
    )
```

profile of v0, /device:TPU:1, one launch (start us, length us, event | category | flops | bytes accessed | tf_op | source)
XLA Modules:
  0.0 1235.9 jit_solution(7251413055012605955)
XLA Ops:
  6.5 0.0 all-gather.11.cloned.1.call-start
  6.5 0.7 all-gather.11.cloned.1.call-update
  7.3 0.0 all-gather.7.cloned.1.call-start
  7.3 1.5 pad_maximum_fusion
  8.8 0.0 all-gather.7.cloned.1.call-update
  8.9 0.0 all-gather.9.cloned.1.call-start
  8.9 5.0 collective-permute-start
  14.0 14.2 %all-gather = bf16[1,128,1024]{2,1,0:T(8,128)(2,1)} all-gather(bf16[1,32,1024]{2,1,0:T(8,128)(2,1)} %param.19), channel_id=2, replica_groups=mesh['row'=16,'col_0'=8,'col_1'=4] {'col_1'}, dimensions={1}, use_global_device_ids=true | all-gather | bytes 327680 | tf_op jit(solution)/shard_map/all_gather | solution.py:33
  28.2 0.0 all-gather.9.cloned.1.call-update
  28.3 0.7 copy.13
  29.0 0.1 reduce-window.9
  29.1 0.1 reduce
  29.2 0.7 sub.362
  29.8 0.8 fusion.52
  30.6 2.2 select_bitcast_fusion
  32.9 0.1 select_reduce_fusion
  33.0 0.1 slice.23
  33.0 0.0 collective-permute-done
  33.0 0.1 slice.21
  33.1 0.0 copy-done.3
  33.1 0.1 compare_and_fusion
  33.2 0.1 compare_select_fusion
  33.3 1049.4 %all-gather.11.cloned.1.call-done = bf16[512,2,1024]{2,1,0:T(2,128)(2,1)} async-done(((bf16[1,2,1024]{2,1,0:T(2,128)(2,1)}), bf16[512,2,1024]{2,1,0:T(2,128)(2,1)}) %all-gather.11.cloned.1.call-update) | async-done | bytes 2097168 | tf_op jit(solution)/shard_map/all_gather | solution.py:100
  1082.7 2.7 reshape.388
  1085.4 2.8 gather_fusion
  1088.2 1.7 multiply_reduce_fusion
  1089.9 1.6 multiply_convert_fusion
  1091.5 0.0 copy-start
  1091.5 125.7 %while.17 = (s32[]{:T(128)}, f32[256,1024]{1,0:T(8,128)S(1)}, s32[256]{0:T(256)S(1)}, bf16[511,1024]{1,0:T(8,128)(2,1)S(1)}, f32[256,1024]{1,0:T(8,128)}, /*inde...) while((s32[]{:T(128)}, f32[256,1024]{1,0:T(8,128)S(1)}, ...), condition=%wide.region_4.5_spmd.clone, body=%wide.region_3.4_spmd.clone.sunk | while | flops 33825024 | bytes 19289948 | solution.py:71
  1091.6 1.3 constant_dynamic-slice_fusion.35
  1093.0 1.4 constant_dynamic-slice_fusion.34
  1094.8 12.2 select_add_fusion.3
  1107.2 1.4 constant_dynamic-slice_fusion.35
  1108.7 1.5 constant_dynamic-slice_fusion.34
  1110.5 12.2 select_add_fusion.3
  1122.8 1.5 constant_dynamic-slice_fusion.35
  1124.4 1.4 constant_dynamic-slice_fusion.34
  1126.2 12.2 select_add_fusion.3
  1138.5 1.5 constant_dynamic-slice_fusion.35
  1140.1 1.4 constant_dynamic-slice_fusion.34
  1141.9 12.2 select_add_fusion.3
  1154.2 1.4 constant_dynamic-slice_fusion.35
  1155.8 1.7 constant_dynamic-slice_fusion.34
  1157.8 12.2 select_add_fusion.3
  1170.1 1.4 constant_dynamic-slice_fusion.35
  1171.6 1.7 constant_dynamic-slice_fusion.34
  1173.7 12.2 select_add_fusion.3
  1186.0 1.3 constant_dynamic-slice_fusion.35
  1187.4 1.7 constant_dynamic-slice_fusion.34
  1189.5 12.2 select_add_fusion.3
  1201.8 1.3 constant_dynamic-slice_fusion.35
  1203.2 1.4 constant_dynamic-slice_fusion.34
  1205.0 12.2 select_add_fusion.3
  1217.2 0.0 copy-done
  1217.2 0.2 fusion.51
  1217.4 0.0 copy-start.1
  1217.5 1.3 copy-done.1
  1218.8 0.3 multiply_reduce_fusion.1
  1219.1 0.0 all-gather.7.cloned.1.call-done
  1219.1 0.0 copy-start.2
  1219.1 3.9 fusion.26
  1223.0 1.6 all-gather.9.cloned.1.call-done
  1224.6 0.0 copy-done.2
  1224.6 4.8 fusion.39
  (23 shorter events, 0.6 us)
Async XLA Ops:
  6.5 26.6 %copy-start.3 = (s32[256]{0:T(256)S(1)}, s32[256]{0:T(256)}, u32[]{:S(2)}) copy-start(s32[256]{0:T(256)} %param.11) | copy-start | bytes 3076
  6.5 1076.1 %all-gather.11.cloned.1.call-start = ((), (), s32[]{:S(2)}) async-start(), calls=%async_computation.2 | async-start | bytes 2101248 | tf_op jit(solution)/shard_map/all_gather | solution.py:100
  7.3 1211.8 %all-gather.7.cloned.1.call-start = ((), (), s32[]{:S(2)}) async-start(), calls=%async_computation | async-start | bytes 4325376 | tf_op jit(solution)/shard_map/all_gather | solution.py:23
  8.9 1215.7 %all-gather.9.cloned.1.call-start = ((), (), s32[]{:S(2)}) async-start(), calls=%async_computation.1 | async-start | bytes 2359296 | tf_op jit(solution)/shard_map/all_gather | solution.py:33
  8.9 24.1 %collective-permute-start = (s32[256]{0:T(256)}, s32[256]{0:T(256)S(1)}, u32[]{:S(2)}, u32[]{:S(2)}) collective-permute-start(s32[256]{0:T(256)} %param.11), channel_id=1, source_target_pairs={{0,1},{1,2},{2,3},{3,4},{4,5},{5,6},{6,7},{7,8},{8,9},{9,10},{10,1... | collective-permute-start | bytes 3080 | tf_op jit(solution)/shard_map/ppermute | solution.py:18
  1091.5 125.7 %copy-start = (bf16[511,1024]{1,0:T(8,128)(2,1)S(1)}, bf16[511,1024]{1,0:T(8,128)(2,1)}, u32[]{:S(2)}) copy-start(bf16[511,1024]{1,0:T(8,128)(2,1)} %gather_fusion) | copy-start | bytes 3139588
  1217.4 1.3 copy-start.1
  1219.1 5.5 copy-start.2
Sparse Core Ops, SparseCore 0:
  9.5 1073.1 all-gather.10
  1085.8 98.4 all-gather.6
  1186.4 38.1 all-gather.8
where the time goes:
time: 1240 us
  waiting for transfers between devices  1050 us (85%)
  other arithmetic  107 us (9%)
  local copies, waits for them, and re-layouts  31.9 us (3%)
  blocking collectives  14.2 us (1%)
  between operations  13.2 us (1%)
    all_gather x1, waiting for transfers between devices, body(): catalogue_all = lax.all_gather(catalogue, ROW_COL, axis=0, tiled=True)  1050 us
    add x8, other arithmetic, one_group(): accumulated = accumulated + jnp.where(keep, shifted * weights, 0.0)  97.5 us
  transfers between devices with their start and end apart: 4, of which 2 were waited for; matrix products, arithmetic and copies ran while one was open for 11% of the time, Pallas kernels for 0%

commit v1 on v0

v1 whole, which is shorter than its diff:
```python
import functools
import jax
import jax.numpy as jnp
from jax import lax
from jax.experimental import pallas as pl
from jax.experimental.pallas import tpu as pltpu
from jax.sharding import Mesh
from jax.sharding import PartitionSpec as P

BF = jnp.bfloat16
F32 = jnp.float32
EPS = 1e-6
MESH = pl.DeviceIdType.MESH


SIZES = (("x", 4), ("yl", 2), ("c", 2), ("z", 8), ("yh", 4))
N_SEM = 224


class Net:
    def __init__(self, send, recv):
        self.send_sem, self.recv_sem, self.used, self.open = send, recv, 0, []
        self.at = {n: lax.axis_index(n) for n, _ in SIZES}

    def peer(self, **other):
        return {n: other.get(n, self.at[n]) for n, _ in SIZES}

    def step(self, distance):
        flat = jnp.int32(0)
        for n, size in SIZES:
            flat = flat * size + self.at[n]
        flat = lax.rem(flat + distance + 512, 512)
        out = {}
        for n, size in reversed(SIZES):
            out[n] = lax.rem(flat, size)
            flat = flat // size
        return out

    def copy(self, src, dst, to):
        k = self.used
        self.used += 1
        one = pltpu.make_async_remote_copy(
            src_ref=src, dst_ref=dst, send_sem=self.send_sem.at[k], recv_sem=self.recv_sem.at[k],
            device_id=to, device_id_type=MESH)
        one.start()
        self.open.append(one)
        return one

    def finish(self):
        for one in self.open:
            one.wait_send()


def geometry(net):
    a = net.at
    d = 2 * a["yl"] - 1
    e = 2 * lax.rem(a["z"], 2) - 1
    g = {}
    g["d"], g["e"] = d, e
    g["y_far"] = net.peer(yh=lax.rem(a["yh"] + d + 4, 4), yl=1 - a["yl"])
    g["y_near"] = net.peer(yl=1 - a["yl"])
    g["z_far"] = net.peer(z=lax.rem(a["z"] + e + 8, 8))
    g["z_near"] = net.peer(z=lax.rem(a["z"] - e + 8, 8))
    g["z_up"] = net.peer(z=lax.rem(a["z"] + 1, 8))
    g["z_down"] = net.peer(z=lax.rem(a["z"] + 7, 8))
    g["twin"] = net.peer(c=1 - a["c"])
    g["xs"] = [net.peer(x=lax.rem(a["x"] + s, 4)) for s in (1, 3, 2)]
    zh = a["z"] // 2
    g["zh"] = zh
    g["group"] = []
    for dc in range(2):
        for dz in range(2):
            for dy in range(4):
                if dc or dz or dy:
                    g["group"].append(net.peer(
                        c=lax.rem(a["c"] + dc, 2), z=2 * zh + lax.rem(a["z"] + dz, 2), yh=lax.rem(a["yh"] + dy, 4)))
    g["next"], g["prev"] = net.step(1), net.step(-1)
    return g


def entry(g):
    barrier = pltpu.get_barrier_semaphore()
    near = g["group"] + g["xs"] + [g["y_far"], g["y_near"], g["z_far"], g["z_near"], g["next"], g["prev"]]
    for to in near:
        pl.semaphore_signal(barrier, inc=1, device_id=to, device_id_type=MESH)
    pl.semaphore_wait(barrier, len(near))


def pair_ring(block, h, d, count, far, near, net):
    one = net.copy(block(h, True), block(h, False), far)
    yield
    one.wait_recv()
    key = lax.rem(h + d + count, count)
    net.share(block(key, False))
    one = net.copy(block(key, False), block(key, False), near)
    yield
    one.wait_recv()
    key = lax.rem(h - d + count, count)
    net.share(block(key, False))
    one = net.copy(block(key, False), block(key, False), far)
    yield
    one.wait_recv()
    net.share(block(lax.rem(h + 2, count), False))


def ring_of_8(block, z, c, up, down, net):
    a = net.copy(block(z, True), block(z, False), up)
    b = net.copy(block(z, True), block(z, False), down)
    yield
    for hop in (1, 2):
        a.wait_recv()
        key = lax.rem(z - hop + 8, 8)
        net.share(block(key, False))
        a = net.copy(block(key, False), block(key, False), up)
        b.wait_recv()
        key = lax.rem(z + hop, 8)
        net.share(block(key, False))
        b = net.copy(block(key, False), block(key, False), down)
        yield
    a.wait_recv()
    net.share(block(lax.rem(z - 3 + 8, 8), False))
    b.wait_recv()
    net.share(block(lax.rem(z + 3, 8), False))
    key = lax.rem(z - 3 + 6 * c + 8, 8)
    to = {n: jnp.where(c == 0, up[n], down[n]) for n in up}
    a = net.copy(block(key, False), block(key, False), to)
    yield
    a.wait_recv()
    net.share(block(lax.rem(z + 4, 8), False))


def gather_kernel(ids_ref, cat_ref, gate_ref, up_ref, down_ref, ids_out, catb, wb, pairs, fill_sem, send, recv):
    net = Net(send, recv)
    g = geometry(net)
    shared = []
    net.share = lambda ref: shared.append(net.copy(ref, ref, g["twin"]))
    a = net.at
    x, yl, c, z, yh, zh = a["x"], a["yl"], a["c"], a["z"], a["yh"], g["zh"]
    fill = []
    for n, ref in enumerate((gate_ref, up_ref, down_ref)):
        for t in range(8):
            one = pltpu.make_async_copy(ref.at[:, 128 * t:128 * t + 128], wb.at[t, n, z, yh], fill_sem.at[8 * n + t])
            one.start()
            fill.append(one)
    entry(g)

    lanes = pl.ds(4 * c, 4)

    def w_y_first(t):
        lt = 4 * c + t
        yield from pair_ring(lambda h, _: wb.at[lt, :, z, h], yh, g["d"], 4, g["y_far"], g["y_near"], net)
        yield from ring_of_8(lambda k, _: wb.at[lt, :, k], z, c, g["z_up"], g["z_down"], net)

    def w_z_first(t):
        lt = 4 * c + t
        yield from ring_of_8(lambda k, _: wb.at[lt, :, k, yh], z, c, g["z_up"], g["z_down"], net)
        yield from pair_ring(lambda h, _: wb.at[lt, :, :, h], yh, g["d"], 4, g["y_far"], g["y_near"], net)

    def cat_x():
        net.share(catb.at[lanes, x, yl, :, zh])
        ref = catb.at[lanes, x, yl, :, zh]
        out = [net.copy(ref, ref, to) for to in g["xs"]]
        yield
        for one, s in zip(out, (1, 3, 2)):
            one.wait_recv()
            net.share(catb.at[lanes, lax.rem(x - s + 4, 4), yl, :, zh])

    def swap_y(part, span):
        send_far = pl.ds(0, 2)
        send_near = pl.ds(2, 2)
        one = net.copy(part(send_far, yl, span), part(send_far, yl, span), g["y_far"])
        two = net.copy(part(send_near, yl, span), part(send_near, yl, span), g["y_near"])
        yield
        one.wait_recv()
        two.wait_recv()
        net.share(part(pl.ds(0, 4), 1 - yl, span))

    def cat_y_first():
        la = pl.ds(4 * c, 2)
        yield from swap_y(lambda xs, k, s: catb.at[la, xs, k, :, s], zh)
        yield from pair_ring(lambda h, _: catb.at[la, :, :, :, h], zh, g["e"], 4, g["z_far"], g["z_near"], net)

    def cat_z_first():
        la = pl.ds(4 * c + 2, 2)
        yield from pair_ring(lambda h, _: catb.at[la, :, yl, :, h], zh, g["e"], 4, g["z_far"], g["z_near"], net)
        yield from swap_y(lambda xs, k, s: catb.at[la, xs, k], None)

    mine = 4 * lax.rem(z, 2) + yh
    group = []
    for to in g["group"]:
        half = pl.ds(pl.multiple_of(512 * to["c"], 512), 512)
        group.append(net.copy(cat_ref.at[:, half], pairs.at[c, mine], to))
    ids = net.copy(ids_ref, ids_out.at[0], g["next"])
    ids_out[1] = ids_ref[...]
    pairs[c, mine] = jnp.where(c == 0, cat_ref[:, 0:512], cat_ref[:, 512:1024])
    for one in fill:
        one.wait()
    weights = [w_y_first(0), w_z_first(2), w_y_first(1), w_z_first(3)]
    for f in weights:
        next(f)
    for one in group:
        one.wait_recv()
    for k in range(2):
        rows = jnp.concatenate([pairs[k, i].astype(F32) for i in range(8)], axis=0).astype(BF)
        for t in range(4):
            catb[4 * c + t, x, yl, k, zh] = rows[:, 128 * t:128 * t + 128]
    def run(flow):
        for _ in flow:
            pass

    run(cat_x())
    flows = [cat_y_first(), cat_z_first()] + weights
    while flows:
        for f in list(flows):
            try:
                next(f)
            except StopIteration:
                flows.remove(f)
    ids.wait_recv()
    for one in shared:
        one.wait_recv()
    net.finish()


def gather(ids, cat, gate, up, down):
    vm = pl.BlockSpec(memory_space=pltpu.VMEM)
    return pl.pallas_call(
        gather_kernel,
        out_shape=(jax.ShapeDtypeStruct((2, 1, 256), jnp.int32),
                   jax.ShapeDtypeStruct((8, 4, 2, 2, 4, 16, 128), BF),
                   jax.ShapeDtypeStruct((8, 3, 8, 4, 32, 128), BF)),
        in_specs=[vm] * 2 + [pl.BlockSpec(memory_space=pl.ANY)] * 3,
        out_specs=(vm,) * 3,
        scratch_shapes=[pltpu.VMEM((2, 8, 2, 512), BF), pltpu.SemaphoreType.DMA((24,)),
                        pltpu.SemaphoreType.DMA((N_SEM,)), pltpu.SemaphoreType.DMA((N_SEM,))],
        compiler_params=pltpu.CompilerParams(collective_id=0, has_side_effects=True, vmem_limit_bytes=40 * 2**20),
    )(ids, cat, gate, up, down)


NT = (((1,), (1,)), ((), ()))


def dot(a, b):
    return jnp.dot(a, b, preferred_element_type=F32)


def dot_nt(a, b):
    return lax.dot_general(a, b, NT, preferred_element_type=F32)


def iota(shape, dim):
    return lax.broadcasted_iota(jnp.int32, shape, dim)


def one(cond):
    return jnp.where(cond, 1.0, 0.0).astype(BF)


def prepare_taps(tl_ref, taps_ref, hr, ht, h):
    p, k = iota((256, 256), 0), iota((256, 256), 1)
    reverse = one(p + k == 256)
    turned = one(k == 16 * (p // 16) + (p % 16 - p // 16 + 16) % 16)
    lag = iota((256, 256), 0)
    for s in range(4):
        cols = slice(256 * s, 256 * s + 256)
        table = jnp.where(lag < tl_ref[:, cols], taps_ref[:, cols].astype(F32), 0.0).astype(BF)
        backward = dot(reverse, table).astype(BF)
        hr[cols, :] = dot_nt(turned, backward).astype(BF)

    def shift_one(j, _):
        shift = one((k == p + j) & (p >= 1))
        for s in range(4):
            rows = dot(hr[256 * s:256 * s + 256, :], shift).astype(BF)
            ht[pl.ds(16 * s, 16), pl.ds(j, 1)] = rows.reshape(16, 1, 16, 256)
        return 0

    lax.fori_loop(0, 16, shift_one, 0)
    unit = one(p == k)

    def flip(g, _):
        for a in range(4):
            h[4 * g + a] = dot_nt(unit, ht[4 * g + a].reshape(256, 256)).astype(BF)
        return 0

    lax.fori_loop(0, 16, flip, 0)


def user_tables(base, len_ref, keep, first, live):
    pos = base + iota((256, 128), 0)
    begin = jnp.zeros((256, 128), jnp.int32)
    pos_b = base + 16 * iota((16, 256), 0)
    begin_b = jnp.zeros((16, 256), jnp.int32)
    start = jnp.int32(0)
    for u in range(len_ref.shape[0]):
        begin = jnp.where(pos >= start, start, begin)
        begin_b = jnp.where(pos_b >= start, start, begin_b)
        start = start + len_ref[u]
    reach = jnp.minimum(pos - begin, iota((256, 128), 0) % 16)
    for lag in range(16):
        keep[lag] = jnp.where(lag <= reach, 1.0, 0.0)
    source = pos_b - 256 + iota((16, 256), 1)
    first[...] = jnp.where(source >= begin_b, 1.0, 0.0)
    head = base + 16 * (iota((256, 128), 0) // 16)
    live[...] = jnp.where(begin < head, 1.0, 0.0)


def wide(ref, n):
    return jnp.concatenate([ref[2 * n], ref[2 * n + 1]], axis=1)


def look_up(ids_ref, cat_ref, gains_ref, hid, nf, nt):
    ids = ids_ref[...].astype(F32)
    for half in range(2):
        row = ids[half:half + 1, :]
        column = jnp.broadcast_to(row, (128, 256)).T
        item = iota((256, 128), 1).astype(F32)
        pick = jnp.concatenate([one(column == item + 128.0 * v) for v in range(8)], axis=1)
        rows = jnp.concatenate([dot(pick, wide(cat_ref, n)) for n in range(4)], axis=1)
        if half == 1:
            hid[...] = rows
        scale = lax.rsqrt(jnp.mean(rows * rows, axis=-1, keepdims=True) + EPS)
        normed = (rows * scale * gains_ref[0:1, :]).astype(BF).astype(F32)
        if half == 1:
            nf[16:272, :] = normed
        else:
            nf[0:16, :] = normed[240:256, :]
        nt[:, 256 * half:256 * half + 256] = normed.T


def windows(nt, first, u):
    def one_group(g, _):
        x = nt[pl.ds(16 * g, 16), :]
        for r in range(8):
            y = x if r == 0 else pltpu.roll(x, 512 - 16 * r, 1)
            for i in (r, r + 8):
                at = 0 if i < 8 else 128
                u[g, i] = (y[:, at:at + 256] * first[i:i + 1, :]).astype(BF)
        return 0

    lax.fori_loop(0, 64, one_group, 0)


def far_taps(u, h, live, far):
    lane = iota((256, 256), 1) % 16
    row = iota((256, 256), 0) % 16
    gap = (lane - row + 16) % 16
    t, q = iota((256, 256), 0), iota((256, 256), 1)
    spread = jnp.where(t == 16 * (q % 16) + q // 16, jnp.concatenate([live[...], live[...]], axis=1), 0.0).astype(BF)
    settle = one(q == 16 * ((t // 16 - t % 16 + 16) % 16) + t % 16)
    bit = iota((16, 128), 1)

    def one_block(s, _):
        w = jnp.zeros((256, 256), F32)
        for g in range(16):
            r = dot(u[16 * s + g].reshape(256, 256), h[16 * s + g])
            w = jnp.where(gap == g, r, w)
        halves = []
        for side in range(2):
            x = [w[16 * i:16 * i + 16, 128 * side:128 * side + 128] for i in range(16)]
            for b in range(4):
                step = 1 << b
                z = []
                for i in range(16):
                    if i & step:
                        z.append(jnp.where((bit & step) != 0, x[i], pltpu.roll(x[i ^ step], 128 - step, 1)))
                    else:
                        z.append(jnp.where((bit & step) == 0, x[i], pltpu.roll(x[i ^ step], step, 1)))
                x = z
            halves.append(jnp.concatenate(x, axis=0).astype(BF))
        turned = jnp.concatenate(halves, axis=1)
        far[s] = dot(dot_nt(spread, turned).astype(BF), settle)
        return 0

    lax.fori_loop(0, 4, one_block, 0)


def near_taps(tl_ref, taps_ref, keep, nf, hid, far):
    for s in range(8):
        cols = slice(128 * s, 128 * s + 128)
        w = jnp.where(iota((16, 128), 0) < tl_ref[:, cols], taps_ref[0:16, cols].astype(F32), 0.0)
        side = slice(128 * (s % 2), 128 * (s % 2) + 128)

        def rows(b, _):
            at = pl.multiple_of(64 * b, 64)
            x = nf[pl.ds(at, 80), cols]
            total = hid[pl.ds(at, 64), cols] + far[s // 2, pl.ds(at, 64), side]
            for lag in range(16):
                total = total + x[16 - lag:80 - lag, :] * (keep[lag, pl.ds(at, 64), :] * w[lag:lag + 1, :])
            hid[pl.ds(at, 64), cols] = total
            return 0

        lax.fori_loop(0, 4, rows, 0)


def feed_forward(gains_ref, w_ref, hid, inner, act, out_ref):
    rows = hid[...]
    scale = lax.rsqrt(jnp.mean(rows * rows, axis=-1, keepdims=True) + EPS)
    inner[...] = (rows * scale * gains_ref[1:2, :]).astype(BF)
    for n in range(4):
        cols = slice(256 * n, 256 * n + 256)
        gate = dot(inner[...], wide(w_ref.at[:, 0], n))
        up = dot(inner[...], wide(w_ref.at[:, 1], n))
        act[:, cols] = (gate / (1.0 + jnp.exp(-gate)) * up).astype(BF)
    for n in range(4):
        cols = slice(256 * n, 256 * n + 256)
        out_ref[:, cols] = (hid[:, cols] + dot(act[...], wide(w_ref.at[:, 2], n))).astype(BF)


def kernel(len_ref, ids_ref, tl_ref, taps_ref, gains_ref, cat_ref, w_ref,
           out_ref, hr, ht, h, keep, first, live, hid, nf, nt, u, far, inner, act):
    base = jnp.int32(0)
    for n, size in SIZES:
        base = base * size + lax.axis_index(n)
    base = base * 256
    prepare_taps(tl_ref, taps_ref, hr, ht, h)
    user_tables(base, len_ref, keep, first, live)
    look_up(ids_ref, cat_ref, gains_ref, hid, nf, nt)
    windows(nt, first, u)
    far_taps(u, h, live, far)
    near_taps(tl_ref, taps_ref, keep, nf, hid, far)
    feed_forward(gains_ref, w_ref, hid, inner, act, out_ref)


SCRATCH = [
    pltpu.VMEM((1024, 256), BF),
    pltpu.VMEM((64, 16, 16, 256), BF),
    pltpu.VMEM((64, 256, 256), BF),
    pltpu.VMEM((16, 256, 128), F32),
    pltpu.VMEM((16, 256), F32),
    pltpu.VMEM((256, 128), F32),
    pltpu.VMEM((256, 1024), F32),
    pltpu.VMEM((272, 1024), F32),
    pltpu.VMEM((1024, 512), F32),
    pltpu.VMEM((64, 16, 16, 256), BF),
    pltpu.VMEM((4, 256, 256), F32),
    pltpu.VMEM((256, 1024), BF),
    pltpu.VMEM((256, 1024), BF),
]


def compute(lens, ids2, tl, taps, gains, cat, w):
    vm = pl.BlockSpec(memory_space=pltpu.VMEM)
    sm = pl.BlockSpec(memory_space=pltpu.SMEM)
    return pl.pallas_call(
        kernel,
        out_shape=jax.ShapeDtypeStruct((256, 1024), BF),
        in_specs=[sm] + [vm] * 6,
        out_specs=vm,
        scratch_shapes=SCRATCH,
        compiler_params=pltpu.CompilerParams(vmem_limit_bytes=60 * 2**20),
    )(lens, ids2, tl, taps, gains, cat, w)


def body(item_ids, user_lengths, catalogue, tap_lengths, conv_taps, norm_gains, gate_weight, up_weight, down_weight):
    ids, catb, wb = gather(item_ids.reshape(1, 256), catalogue, gate_weight[0], up_weight[0], down_weight[0])
    return compute(user_lengths, ids.reshape(2, 256), tap_lengths, conv_taps[0], norm_gains[0],
                   catb.reshape(8, 1024, 128), wb.reshape(8, 3, 1024, 128))


def solution(mesh):
    finer = Mesh(mesh.devices.reshape([size for _, size in SIZES]), [name for name, _ in SIZES])
    every, col = ("x", "yl", "c", "z", "yh"), ("z", "yh")
    placed = (P(every), P(), P(every, None), P(), P(), P(), P(None, col, None), P(None, col, None), P(None, col, None))
    return jax.shard_map(body, mesh=finer, in_specs=placed, out_specs=P(every, None), check_vma=False)
```

time: 1240 us -> 112 us (0.09)
  waiting for transfers between devices: 1050 us -> 0 us
  other arithmetic: 107 us -> 0 us
  Pallas kernels: 0 us -> 103 us
  local copies, waits for them, and re-layouts: 31.9 us -> 8.46 us
  blocking collectives: 14.2 us -> 0 us
  between operations: 13.2 us -> 0.02 us
    all_gather x3 -> x0, waiting for transfers between devices: 1050 us -> none  [the longest x1 1050 us: body(): catalogue_all = lax.all_gather(catalogue, ROW_COL, axis=0, tiled=True)]
    pallas_call x0 -> x2, Pallas kernels: none -> 103 us  [the longest x1 64.9 us: gather(): pl.pallas_call(gather_kernel, out_shape=(jax.ShapeDtypeStruct((2, 1, 256)...]
    add x9 -> x0, other arithmetic: 97.5 us -> none  [the longest x8 97.5 us: one_group(): accumulated = accumulated + jnp.where(keep, shifted * weights, 0.0)]
    dynamic_slice x16 -> x0, local copies, waits for them, and re-layouts: 23.4 us -> none  [one_group(): weights = lax.dynamic_slice_in_dim(tap_table, lag_index, 1, 0)]
    all_gather x1 -> x0, blocking collectives: 14.2 us -> none  [whole_of(): result = lax.all_gather(result, axes[number], axis=dim, tiled=True)]
  transfers between devices with their start and end apart: 4 -> 0, of which waited for: 2 -> 0; matrix products, arithmetic and copies ran while one was open for 11% -> 0% of each run, Pallas kernels for 0% -> 0%
where the time goes in v1:
time: 112 us
  Pallas kernels  103 us (92%)
  local copies, waits for them, and re-layouts  8.46 us (8%)
    pallas_call x1, Pallas kernels, gather(): pl.pallas_call(gather_kernel, out_shape=(jax.ShapeDtypeStruct((2, 1, 256)...  64.9 us
    pallas_call x1, Pallas kernels, compute(): pl.pallas_call(kernel, out_shape=jax.ShapeDtypeStruct((256, 1024), BF), i...  38.2 us
    unnamed x15, local copies, waits for them, and re-layouts  8.46 us

profile of v1, /device:TPU:1, one launch (start us, length us, event | category | flops | bytes accessed | tf_op | source)
XLA Modules:
  0.0 111.5 jit_solution(15503348446752091109)
XLA Ops:
  0.0 0.0 copy-start.2
  0.0 0.8 copy-done.2
  0.8 0.0 copy-start.3
  0.8 0.8 copy-done.3
  1.7 0.0 copy-start.4
  1.7 0.8 copy-done.4
  2.5 0.0 copy-start.5
  2.5 0.7 copy-done.5
  3.2 0.0 copy-start.6
  3.2 0.7 copy-done.6
  3.9 64.9 %shard_map.91 = (s32[2,1,256]{2,1,0:T(1,128)S(1)}, bf16[8,4,2,2,4,16,128]{6,5,4,3,2,1,0:T(8,128)(2,1)S(1)}, bf16[8,3,8,4,32,128]{5,4,3,2,1,0:T(8,128)(2,1)S(1)}) custom-call(s32[1,256]{1,0:T(1,128)S(1)} %bitcast.16, bf16[2,1024]{1,0:T(2,128)(2,1)S(1)} %copy-done.5, bf16[32,1024]{1,0:T(8,128)(2,1)S(1)} %bitcast.13, bf16[32,1024]{1,0:T(8,128)(2,1)S(1)} %bitcast.14, ...), custom_call_target="tpu_custom_call" | custom-call | tf_op jit(solution)/shard_map/pallas_call | solution.py:227
  68.8 0.0 copy-start
  68.8 2.6 %copy-done = bf16[8,3,8,4,32,128]{5,4,3,2,1,0:T(8,128)(2,1)} copy-done((bf16[8,3,8,4,32,128]{5,4,3,2,1,0:T(8,128)(2,1)}, bf16[8,3,8,4,32,128]{5,4,3,2,1,0:T(8,128)(2,1)S(1)}, u32[]{:S(2)}) %copy-start) | copy-done | bytes 6291480
  71.4 0.0 copy-start.1
  71.4 1.4 %copy-done.1 = bf16[8,4,2,2,4,16,128]{6,5,4,3,2,1,0:T(8,128)(2,1)} copy-done((bf16[8,4,2,2,4,16,128]{6,5,4,3,2,1,0:T(8,128)(2,1)}, bf16[8,4,2,2,4,16,128]{6,5,4,3,2,1,0:T(8,128)(2,1)S(1)}, u32[]{:S(2)}) %copy-start.1) | copy-done | bytes 2097176
  72.8 0.6 copy.12
  73.4 38.2 %shard_map.92 = bf16[256,1024]{1,0:T(8,128)(2,1)} custom-call(s32[32]{0:T(128)} %len_ref.1, s32[2,256]{1,0:T(2,128)} %bitcast.19, s32[1,1024]{1,0:T(1,128)} %tl_ref.1, bf16[256,1024]{1,0:T(8,128)(2,1)} %bitcast.17, f32[2,1024]{1,0:T(2,128)} %bitcast.18, bf16[8,1024,128]{2,1,0:T(8,128)(2,1)} %bitcast.12, bf16[8,3,1024,128]{3,2,1,0:T(8,128)(2,1)} %bitcast.11), custom_call_target="tpu_custom_call" | custom-call | tf_op jit(solution)/shard_map/pallas_call | solution.py:444
Async XLA Ops:
  0.0 0.8 copy-start.2
  0.8 0.8 copy-start.3
  1.7 0.8 copy-start.4
  2.5 0.7 copy-start.5
  3.2 0.7 copy-start.6
  68.8 2.7 %copy-start = (bf16[8,3,8,4,32,128]{5,4,3,2,1,0:T(8,128)(2,1)}, bf16[8,3,8,4,32,128]{5,4,3,2,1,0:T(8,128)(2,1)S(1)}, u32[]{:S(2)}) copy-start(bf16[8,3,8,4,32,128]{5,4,3,2,1,0:T(8,128)(2,1)S(1)} %get-tuple-element.10) | copy-start | bytes 18874372
  71.4 1.4 %copy-start.1 = (bf16[8,4,2,2,4,16,128]{6,5,4,3,2,1,0:T(8,128)(2,1)}, bf16[8,4,2,2,4,16,128]{6,5,4,3,2,1,0:T(8,128)(2,1)S(1)}, u32[]{:S(2)}) copy-start(bf16[8,4,2,2,4,16,128]{6,5,4,3,2,1,0:T(8,128)(2,1)S(1)} %get-tuple-element.9) | copy-start | bytes 6291460

commit v2 on v1

v2 whole, which is shorter than its diff:
```python
import jax
import jax.numpy as jnp
from jax import lax
from jax.experimental import pallas as pl
from jax.experimental.pallas import tpu as pltpu
from jax.sharding import Mesh
from jax.sharding import PartitionSpec as P

BF = jnp.bfloat16
F32 = jnp.float32
EPS = 1e-6
MESH = pl.DeviceIdType.MESH
NT = (((1,), (1,)), ((), ()))
SIZES = (("x", 4), ("yl", 2), ("c", 2), ("z", 8), ("yh", 4))
N_SEM = 224


class Net:
    def __init__(self, send, recv):
        self.send_sem, self.recv_sem, self.used, self.open = send, recv, 0, []
        self.at = {n: lax.axis_index(n) for n, _ in SIZES}

    def peer(self, **other):
        return {n: other.get(n, self.at[n]) for n, _ in SIZES}

    def step(self, distance):
        flat = jnp.int32(0)
        for n, size in SIZES:
            flat = flat * size + self.at[n]
        flat = lax.rem(flat + distance + 512, 512)
        out = {}
        for n, size in reversed(SIZES):
            out[n] = lax.rem(flat, size)
            flat = flat // size
        return out

    def copy(self, src, dst, to):
        k = self.used
        self.used += 1
        one = pltpu.make_async_remote_copy(
            src_ref=src, dst_ref=dst, send_sem=self.send_sem.at[k], recv_sem=self.recv_sem.at[k],
            device_id=to, device_id_type=MESH)
        one.start()
        self.open.append(one)
        return one

    def finish(self):
        for one in self.open:
            one.wait_send()


def geometry(net):
    a = net.at
    d = 2 * a["yl"] - 1
    e = 2 * lax.rem(a["z"], 2) - 1
    g = {}
    g["d"], g["e"] = d, e
    g["y_far"] = net.peer(yh=lax.rem(a["yh"] + d + 4, 4), yl=1 - a["yl"])
    g["y_near"] = net.peer(yl=1 - a["yl"])
    g["z_far"] = net.peer(z=lax.rem(a["z"] + e + 8, 8))
    g["z_near"] = net.peer(z=lax.rem(a["z"] - e + 8, 8))
    g["z_up"] = net.peer(z=lax.rem(a["z"] + 1, 8))
    g["z_down"] = net.peer(z=lax.rem(a["z"] + 7, 8))
    y = 2 * a["yh"] + a["yl"]
    up, down = lax.rem(y + 1, 8), lax.rem(y + 7, 8)
    g["y"] = y
    g["y_up"] = net.peer(yh=up // 2, yl=lax.rem(up, 2))
    g["y_down"] = net.peer(yh=down // 2, yl=lax.rem(down, 2))
    g["twin"] = net.peer(c=1 - a["c"])
    g["xs"] = [net.peer(x=lax.rem(a["x"] + s, 4)) for s in (1, 3, 2)]
    zh = a["z"] // 2
    g["zh"] = zh
    g["group"] = []
    for dc in range(2):
        for dz in range(2):
            for dy in range(4):
                if dc or dz or dy:
                    g["group"].append(net.peer(
                        c=lax.rem(a["c"] + dc, 2), z=2 * zh + lax.rem(a["z"] + dz, 2), yh=lax.rem(a["yh"] + dy, 4)))
    g["next"], g["prev"] = net.step(1), net.step(-1)
    return g


def entry_signals(g):
    barrier = pltpu.get_barrier_semaphore()
    near = g["group"] + g["xs"] + [g["y_far"], g["y_near"], g["z_far"], g["z_near"], g["y_up"], g["y_down"], g["z_up"], g["z_down"], g["next"], g["prev"]]
    for to in near:
        pl.semaphore_signal(barrier, inc=1, device_id=to, device_id_type=MESH)
    return len(near)


def pair_ring(block, h, d, count, far, near, net):
    one = net.copy(block(h), block(h), far)
    yield
    one.wait_recv()
    key = lax.rem(h + d + count, count)
    net.share_cat(block(key))
    one = net.copy(block(key), block(key), near)
    yield
    one.wait_recv()
    key = lax.rem(h - d + count, count)
    net.share_cat(block(key))
    one = net.copy(block(key), block(key), far)
    yield
    one.wait_recv()
    net.share_cat(block(lax.rem(h + 2, count)))


def ring_of_8(block, z, c, up, down, net):
    a = net.copy(block(z), block(z), up)
    b = net.copy(block(z), block(z), down)
    yield
    for hop in (1, 2):
        a.wait_recv()
        key = lax.rem(z - hop + 8, 8)
        net.share(block(key))
        a = net.copy(block(key), block(key), up)
        b.wait_recv()
        key = lax.rem(z + hop, 8)
        net.share(block(key))
        b = net.copy(block(key), block(key), down)
        yield
    a.wait_recv()
    net.share(block(lax.rem(z - 3 + 8, 8)))
    b.wait_recv()
    net.share(block(lax.rem(z + 3, 8)))
    key = lax.rem(z - 3 + 6 * c + 8, 8)
    to = {n: jnp.where(c == 0, up[n], down[n]) for n in up}
    a = net.copy(block(key), block(key), to)
    yield
    a.wait_recv()
    net.share(block(lax.rem(z + 4, 8)))


def dot(a, b):
    return jnp.dot(a, b, preferred_element_type=F32)


def dot_nt(a, b):
    return lax.dot_general(a, b, NT, preferred_element_type=F32)


def iota(shape, dim):
    return lax.broadcasted_iota(jnp.int32, shape, dim)


def one(cond):
    return jnp.where(cond, 1.0, 0.0).astype(BF)


def tap_rows(tl, taps, hr):
    p, k = iota((256, 256), 0), iota((256, 256), 1)
    reverse = one(p + k == 256)
    turned = one(k == 16 * (p // 16) + (p % 16 - p // 16 + 16) % 16)
    for s in range(4):
        cols = slice(256 * s, 256 * s + 256)
        table = jnp.where(p < tl[:, cols], taps[:, cols].astype(F32), 0.0).astype(BF)
        hr[cols, :] = dot_nt(turned, dot(reverse, table).astype(BF)).astype(BF)


def tap_shifts(hr, ht, begin, count):
    p, k = iota((256, 256), 0), iota((256, 256), 1)

    def shift_one(j, _):
        shift = one((k == p + j) & (p >= 1))
        for s in range(4):
            rows = dot(hr[256 * s:256 * s + 256, :], shift).astype(BF)
            ht[pl.ds(16 * s, 16), pl.ds(j, 1)] = rows.reshape(16, 1, 16, 256)
        return 0

    lax.fori_loop(begin, begin + count, shift_one, 0)


def tap_flips(ht, h, begin, count):
    unit = one(iota((256, 256), 0) == iota((256, 256), 1))

    def flip(g, _):
        for a in range(4):
            h[4 * g + a] = dot_nt(unit, ht[4 * g + a].reshape(256, 256)).astype(BF)
        return 0

    lax.fori_loop(begin, begin + count, flip, 0)


def user_tables(base, len_ref, keep, first, live):
    pos = base + iota((256, 128), 0)
    begin = jnp.zeros((256, 128), jnp.int32)
    pos_b = base + 16 * iota((16, 256), 0)
    begin_b = jnp.zeros((16, 256), jnp.int32)
    start = jnp.int32(0)
    for u in range(len_ref.shape[0]):
        begin = jnp.where(pos >= start, start, begin)
        begin_b = jnp.where(pos_b >= start, start, begin_b)
        start = start + len_ref[u]
    reach = jnp.minimum(pos - begin, iota((256, 128), 0) % 16)
    for lag in range(16):
        keep[lag] = jnp.where(lag <= reach, 1.0, 0.0)
    source = pos_b - 256 + iota((16, 256), 1)
    first[...] = jnp.where(source >= begin_b, 1.0, 0.0)
    head = base + 16 * (iota((256, 128), 0) // 16)
    live[...] = jnp.where(begin < head, 1.0, 0.0)


def wide(ref, n):
    return jnp.concatenate([ref[2 * n + k].reshape(1024, 128) for k in range(2)], axis=1)


def look_up(ids_ref, cat_ref, gains_ref, hid, nf, nt):
    ids = ids_ref[...].reshape(2, 256).astype(F32)
    for half in range(2):
        row = ids[half:half + 1, :]
        column = jnp.broadcast_to(row, (128, 256)).T
        item = iota((256, 128), 1).astype(F32)
        pick = jnp.concatenate([one(column == item + 128.0 * v) for v in range(8)], axis=1)
        rows = jnp.concatenate([dot(pick, wide(cat_ref, n)) for n in range(4)], axis=1)
        if half == 1:
            hid[...] = rows
        scale = lax.rsqrt(jnp.mean(rows * rows, axis=-1, keepdims=True) + EPS)
        normed = (rows * scale * gains_ref[0:1, :]).astype(BF).astype(F32)
        if half == 1:
            nf[16:272, :] = normed
        else:
            nf[0:16, :] = normed[240:256, :]
        nt[:, 256 * half:256 * half + 256] = normed.T


def windows(nt, first, u, begin, count):
    def one_group(n, _):
        for a in range(4):
            group(4 * n + a)
        return 0

    def group(g):
        x = nt[pl.ds(16 * g, 16), :]
        for r in range(8):
            y = x if r == 0 else pltpu.roll(x, 512 - 16 * r, 1)
            for i in (r, r + 8):
                at = 0 if i < 8 else 128
                u[g, i] = (y[:, at:at + 256] * first[i:i + 1, :]).astype(BF)

    lax.fori_loop(begin // 4, (begin + count) // 4, one_group, 0)


def far_taps(u, h, live, far, s):
    lane = iota((256, 256), 1) % 16
    row = iota((256, 256), 0) % 16
    gap = (lane - row + 16) % 16
    t, q = iota((256, 256), 0), iota((256, 256), 1)
    spread = jnp.where(t == 16 * (q % 16) + q // 16, jnp.concatenate([live[...], live[...]], axis=1), 0.0).astype(BF)
    settle = one(q == 16 * ((t // 16 - t % 16 + 16) % 16) + t % 16)
    bit = iota((16, 128), 1)

    def one_block():
        w = jnp.zeros((256, 256), F32)
        for g in range(16):
            r = dot(u[16 * s + g].reshape(256, 256), h[16 * s + g])
            w = jnp.where(gap == g, r, w)
        halves = []
        for side in range(2):
            x = [w[16 * i:16 * i + 16, 128 * side:128 * side + 128] for i in range(16)]
            for b in range(4):
                step = 1 << b
                z = []
                for i in range(16):
                    if i & step:
                        z.append(jnp.where((bit & step) != 0, x[i], pltpu.roll(x[i ^ step], 128 - step, 1)))
                    else:
                        z.append(jnp.where((bit & step) == 0, x[i], pltpu.roll(x[i ^ step], step, 1)))
                x = z
            halves.append(jnp.concatenate(x, axis=0).astype(BF))
        turned = jnp.concatenate(halves, axis=1)
        far[s] = dot(dot_nt(spread, turned).astype(BF), settle)

    one_block()


def near_taps(tl_ref, taps_ref, keep, nf, hid, far, parts):
    for s in parts:
        cols = slice(128 * s, 128 * s + 128)
        w = jnp.where(iota((16, 128), 0) < tl_ref[:, cols], taps_ref[0:16, cols].astype(F32), 0.0)
        side = slice(128 * (s % 2), 128 * (s % 2) + 128)

        def rows(b, _):
            at = pl.multiple_of(64 * b, 64)
            x = nf[pl.ds(at, 80), cols]
            total = hid[pl.ds(at, 64), cols] + far[s // 2, pl.ds(at, 64), side]
            for lag in range(16):
                total = total + x[16 - lag:80 - lag, :] * (keep[lag, pl.ds(at, 64), :] * w[lag:lag + 1, :])
            hid[pl.ds(at, 64), cols] = total
            return 0

        lax.fori_loop(0, 4, rows, 0)


def wide_w(ref, a, n):
    return jnp.concatenate([ref[2 * n + k, a].reshape(1024, 128) for k in range(2)], axis=1)


def feed_forward(gains_ref, w_ref, hid, inner, act, out_ref):
    rows = hid[...]
    scale = lax.rsqrt(jnp.mean(rows * rows, axis=-1, keepdims=True) + EPS)
    inner[...] = (rows * scale * gains_ref[1:2, :]).astype(BF)
    for n in range(4):
        cols = slice(256 * n, 256 * n + 256)
        gate = dot(inner[...], wide_w(w_ref, 0, n))
        up = dot(inner[...], wide_w(w_ref, 1, n))
        act[:, cols] = (gate / (1.0 + jnp.exp(-gate)) * up).astype(BF)
    for n in range(4):
        cols = slice(256 * n, 256 * n + 256)
        out_ref[:, cols] = (hid[:, cols] + dot(act[...], wide_w(w_ref, 2, n))).astype(BF)


def flows_of(net, g, catb, wb):
    a = net.at
    x, yl, c, z, yh, zh, y = a["x"], a["yl"], a["c"], a["z"], a["yh"], g["zh"], g["y"]
    lanes = pl.ds(4 * c, 4)

    def w_y_first(t):
        lt = 4 * c + t
        yield from ring_of_8(lambda k: wb.at[lt, :, z, k], y, c, g["y_up"], g["y_down"], net)
        yield from ring_of_8(lambda k: wb.at[lt, :, k], z, c, g["z_up"], g["z_down"], net)

    def w_z_first(t):
        lt = 4 * c + t
        yield from ring_of_8(lambda k: wb.at[lt, :, k, y], z, c, g["z_up"], g["z_down"], net)
        yield from ring_of_8(lambda k: wb.at[lt, :, :, k], y, c, g["y_up"], g["y_down"], net)

    def cat_x():
        net.share_cat(catb.at[lanes, x, yl, :, zh])
        ref = catb.at[lanes, x, yl, :, zh]
        out = [net.copy(ref, ref, to) for to in g["xs"]]
        yield
        for one_copy, s in zip(out, (1, 3, 2)):
            one_copy.wait_recv()
            net.share_cat(catb.at[lanes, lax.rem(x - s + 4, 4), yl, :, zh])

    def swap_y(part):
        first = net.copy(part(pl.ds(0, 2), yl), part(pl.ds(0, 2), yl), g["y_far"])
        second = net.copy(part(pl.ds(2, 2), yl), part(pl.ds(2, 2), yl), g["y_near"])
        yield
        first.wait_recv()
        second.wait_recv()
        net.share_cat(part(pl.ds(0, 4), 1 - yl))

    def cat_y_first():
        la = pl.ds(4 * c, 2)
        yield from swap_y(lambda xs, k: catb.at[la, xs, k, :, zh])
        yield from pair_ring(lambda h: catb.at[la, :, :, :, h], zh, g["e"], 4, g["z_far"], g["z_near"], net)

    def cat_z_first():
        la = pl.ds(4 * c + 2, 2)
        yield from pair_ring(lambda h: catb.at[la, :, yl, :, h], zh, g["e"], 4, g["z_far"], g["z_near"], net)
        yield from swap_y(lambda xs, k: catb.at[la, xs, k])

    return cat_x(), [cat_y_first(), cat_z_first()], [w_y_first(0), w_z_first(2), w_y_first(1), w_z_first(3)]


def tick(flows):
    for f in list(flows):
        try:
            next(f)
        except StopIteration:
            flows.remove(f)


def layer(len_hbm, ids_hbm, tl_hbm, taps_hbm, gains_hbm, cat_hbm, gate_hbm, up_hbm, down_hbm, out_ref,
          lens, ids, tl, taps, gains, pair, pairs, catb, wb, hr, ht, h, keep, first, live, hid, nf, nt, far, inner, act,
          load_sem, fill_sem, send, recv):
    net = Net(send, recv)
    g = geometry(net)
    a = net.at
    x, yl, c, z, yh, zh, y = a["x"], a["yl"], a["c"], a["z"], a["yh"], g["zh"], g["y"]
    loads = []
    for n, (src, dst) in enumerate(((cat_hbm, pair), (ids_hbm, ids.at[1]), (len_hbm, lens), (tl_hbm, tl), (gains_hbm, gains), (taps_hbm, taps))):
        loads.append(pltpu.make_async_copy(src, dst, load_sem.at[n]))
        loads[-1].start()
    fill = []
    mine = pl.ds(pl.multiple_of(16 * yl, 16), 16)
    for n, ref in enumerate((gate_hbm, up_hbm, down_hbm)):
        for t in range(8):
            fill.append(pltpu.make_async_copy(ref.at[mine, 128 * t:128 * t + 128], wb.at[t, n, z, y], fill_sem.at[8 * n + t]))
            fill[-1].start()
    near = entry_signals(g)
    loads[2].wait()
    base = jnp.int32(0)
    for n, size in SIZES:
        base = base * size + a[n]
    base = base * 256
    for k in (0, 1, 3, 4, 5):
        loads[k].wait()
    for one_copy in fill:
        one_copy.wait()
    pl.semaphore_wait(pltpu.get_barrier_semaphore(), near)

    shared, shared_cat = [], []
    net.share = lambda ref: shared.append(net.copy(ref, ref, g["twin"]))
    net.share_cat = lambda ref: shared_cat.append(net.copy(ref, ref, g["twin"]))
    cat_x, cats, weights = flows_of(net, g, catb, wb)
    slot = 4 * lax.rem(z, 2) + yh
    group = []
    for to in g["group"]:
        half = pl.ds(pl.multiple_of(512 * to["c"], 512), 512)
        group.append(net.copy(pair.at[:, half], pairs.at[c, slot], to))
    before = net.copy(ids.at[1], ids.at[0], g["next"])
    pairs[c, slot] = jnp.where(c == 0, pair[:, 0:512], pair[:, 512:1024])
    tick(weights)
    user_tables(base, lens, keep, first, live)
    tap_rows(tl, taps, hr)
    tap_shifts(hr, ht, 0, 2)
    for one_copy in group:
        one_copy.wait_recv()
    for k in range(2):
        rows = jnp.concatenate([pairs[k, i].astype(F32) for i in range(8)], axis=0).astype(BF)
        for t in range(4):
            catb[4 * c + t, x, yl, k, zh] = rows[:, 128 * t:128 * t + 128]
    tick(weights)
    next(cat_x)
    tap_shifts(hr, ht, 2, 5)
    tick([cat_x])
    tick(cats)
    tick(weights)
    tap_shifts(hr, ht, 7, 5)
    tick(cats)
    tick(weights)
    tap_shifts(hr, ht, 12, 4)
    tick(cats)
    tap_flips(ht, h, 0, 8)
    tick(cats)
    tick(weights)
    tap_flips(ht, h, 8, 8)
    tick(cats)
    tick(weights)
    while cats:
        tick(cats)
    before.wait_recv()
    for one_copy in shared_cat:
        one_copy.wait_recv()
    look_up(ids, catb, gains, hid, nf, nt)
    for s in range(4):
        tick(weights)
        windows(nt, first, ht, 16 * s, 16)
        far_taps(ht, h, live, far, s)
    tick(weights)
    near_taps(tl, taps, keep, nf, hid, far, range(8))
    while weights:
        tick(weights)
    for one_copy in shared:
        one_copy.wait_recv()
    feed_forward(gains, wb, hid, inner, act, out_ref)
    net.finish()


def body(item_ids, user_lengths, catalogue, tap_lengths, conv_taps, norm_gains, gate_weight, up_weight, down_weight):
    anywhere = pl.BlockSpec(memory_space=pl.ANY)
    return pl.pallas_call(
        layer,
        out_shape=jax.ShapeDtypeStruct((256, 1024), BF),
        in_specs=[anywhere] * 9,
        out_specs=pl.BlockSpec(memory_space=pltpu.VMEM),
        scratch_shapes=[
            pltpu.SMEM((32,), jnp.int32),
            pltpu.VMEM((2, 1, 256), jnp.int32),
            pltpu.VMEM((1, 1024), jnp.int32),
            pltpu.VMEM((256, 1024), BF),
            pltpu.VMEM((2, 1024), F32),
            pltpu.VMEM((2, 1024), BF),
            pltpu.VMEM((2, 8, 2, 512), BF),
            pltpu.VMEM((8, 4, 2, 2, 4, 16, 128), BF),
            pltpu.VMEM((8, 3, 8, 8, 16, 128), BF),
            pltpu.VMEM((1024, 256), BF),
            pltpu.VMEM((64, 16, 16, 256), BF),
            pltpu.VMEM((64, 256, 256), BF),
            pltpu.VMEM((16, 256, 128), F32),
            pltpu.VMEM((16, 256), F32),
            pltpu.VMEM((256, 128), F32),
            pltpu.VMEM((256, 1024), F32),
            pltpu.VMEM((272, 1024), F32),
            pltpu.VMEM((1024, 512), F32),
            pltpu.VMEM((4, 256, 256), F32),
            pltpu.VMEM((256, 1024), BF),
            pltpu.VMEM((256, 1024), BF),
            pltpu.SemaphoreType.DMA((6,)),
            pltpu.SemaphoreType.DMA((24,)),
            pltpu.SemaphoreType.DMA((N_SEM,)),
            pltpu.SemaphoreType.DMA((N_SEM,)),
        ],
        compiler_params=pltpu.CompilerParams(
            collective_id=0, has_side_effects=True, vmem_limit_bytes=66_000_000),
    )(user_lengths, item_ids.reshape(1, 256), tap_lengths, conv_taps[0], norm_gains[0], catalogue,
      gate_weight[0], up_weight[0], down_weight[0])


def solution(mesh):
    finer = Mesh(mesh.devices.reshape([size for _, size in SIZES]), [name for name, _ in SIZES])
    every, col = ("x", "yl", "c", "z", "yh"), ("z", "yh")
    placed = (P(every), P(), P(every, None), P(), P(), P(), P(None, col, None), P(None, col, None), P(None, col, None))
    return jax.shard_map(body, mesh=finer, in_specs=placed, out_specs=P(every, None), check_vma=False)
```

time: 112 us -> 78.3 us (0.70)
  the two profiles are of different devices: /device:TPU:1 before, /device:TPU:24 now
where the time goes in v2:
time: 78.3 us; the launch traced here: 78.1 us
  Pallas kernels  76.3 us (97%)
  local copies, waits for them, and re-layouts  1.87 us (2%)
    pallas_call x1, Pallas kernels, body(): pl.pallas_call(layer, out_shape=jax.ShapeDtypeStruct((256, 1024), BF), in...  76.3 us
    unnamed x1, local copies, waits for them, and re-layouts  1.87 us

profile of v2, /device:TPU:24, one launch (start us, length us, event | category | flops | bytes accessed | tf_op | source)
XLA Modules:
  0.0 78.1 jit_solution(15763927136763007002)
XLA Ops:
  0.0 76.3 %shard_map.91 = bf16[256,1024]{1,0:T(8,128)(2,1)} custom-call(s32[32]{0:T(128)} %len_hbm.1, s32[1,256]{1,0:T(1,128)} %bitcast.11, s32[1,1024]{1,0:T(1,128)} %tl_hbm.1, bf16[256,1024]{1,0:T(8,128)(2,1)} %bitcast.6, f32[2,1024]{1,0:T(2,128)} %bitcast.10, bf16[2,1024]{1,0:T(2,128)(2,1)} %cat_hbm.1, bf16[32,1024]{1,0:T(8,128)(2,1)} %bitcast.7, ...), custom_call_target="tpu_custom_call" | custom-call | tf_op jit(solution)/shard_map/pallas_call | solution.py:455
  76.3 1.9 %copy.11 = bf16[256,1024]{1,0:T(8,128)(2,1)} copy(bf16[256,1024]{1,0:T(8,128)(2,1)} %shard_map.91) | data formatting | bytes 1048576

commit v3 on v2

--- a/solution.py
+++ b/solution.py
@@ -11,6 +11,9 @@
 EPS = 1e-6
 MESH = pl.DeviceIdType.MESH
 NT = (((1,), (1,)), ((), ()))
+ORDER = "skew"
+NT_DTYPE = BF
+FIRST_DTYPE = BF
 SIZES = (("x", 4), ("yl", 2), ("c", 2), ("z", 8), ("yh", 4))
 N_SEM = 224
 
@@ -66,6 +69,12 @@
     g["y"] = y
     g["y_up"] = net.peer(yh=up // 2, yl=lax.rem(up, 2))
     g["y_down"] = net.peer(yh=down // 2, yl=lax.rem(down, 2))
+    g["ys"], g["zs"] = [], []
+    for s in range(1, 8):
+        to = lax.rem(y + s, 8)
+        g["ys"].append(net.peer(yh=to // 2, yl=lax.rem(to, 2)))
+        g["zs"].append(net.peer(z=lax.rem(a["z"] + s, 8)))
+    g["z_run"] = [net.peer(z=lax.rem(a["z"] + s * e + 8, 8)) for s in (1, 2, 3)]
     g["twin"] = net.peer(c=1 - a["c"])
     g["xs"] = [net.peer(x=lax.rem(a["x"] + s, 4)) for s in (1, 3, 2)]
     zh = a["z"] // 2
@@ -83,7 +92,7 @@
 
 def entry_signals(g):
     barrier = pltpu.get_barrier_semaphore()
-    near = g["group"] + g["xs"] + [g["y_far"], g["y_near"], g["z_far"], g["z_near"], g["y_up"], g["y_down"], g["z_up"], g["z_down"], g["next"], g["prev"]]
+    near = g["group"] + g["xs"] + g["ys"] + g["zs"] + [g["next"], g["prev"]]
     for to in near:
         pl.semaphore_signal(barrier, inc=1, device_id=to, device_id_type=MESH)
     return len(near)
@@ -196,7 +205,7 @@
     for lag in range(16):
         keep[lag] = jnp.where(lag <= reach, 1.0, 0.0)
     source = pos_b - 256 + iota((16, 256), 1)
-    first[...] = jnp.where(source >= begin_b, 1.0, 0.0)
+    first[...] = jnp.where(source >= begin_b, 1.0, 0.0).astype(BF)
     head = base + 16 * (iota((256, 128), 0) // 16)
     live[...] = jnp.where(begin < head, 1.0, 0.0)
 
@@ -221,7 +230,7 @@
             nf[16:272, :] = normed
         else:
             nf[0:16, :] = normed[240:256, :]
-        nt[:, 256 * half:256 * half + 256] = normed.T
+        nt[:, 256 * half:256 * half + 256] = normed.astype(BF).T
 
 
 def windows(nt, first, u, begin, count):
@@ -236,9 +245,10 @@
             y = x if r == 0 else pltpu.roll(x, 512 - 16 * r, 1)
             for i in (r, r + 8):
                 at = 0 if i < 8 else 128
-                u[g, i] = (y[:, at:at + 256] * first[i:i + 1, :]).astype(BF)
-
-    lax.fori_loop(begin // 4, (begin + count) // 4, one_group, 0)
+                u[g, i] = y[:, at:at + 256] * first[i:i + 1, :]
+
+    for n in range(begin // 4, (begin + count) // 4):
+        one_group(n, 0)
 
 
 def far_taps(u, h, live, far, s):
@@ -274,30 +284,26 @@
     one_block()
 
 
-def near_taps(tl_ref, taps_ref, keep, nf, hid, far, parts):
+def near_taps(tl_ref, taps_ref, keep, nf, hid, parts):
     for s in parts:
         cols = slice(128 * s, 128 * s + 128)
         w = jnp.where(iota((16, 128), 0) < tl_ref[:, cols], taps_ref[0:16, cols].astype(F32), 0.0)
-        side = slice(128 * (s % 2), 128 * (s % 2) + 128)
-
-        def rows(b, _):
-            at = pl.multiple_of(64 * b, 64)
-            x = nf[pl.ds(at, 80), cols]
-            total = hid[pl.ds(at, 64), cols] + far[s // 2, pl.ds(at, 64), side]
+        for b in range(4):
+            rows = slice(64 * b, 64 * b + 64)
+            x = nf[64 * b:64 * b + 80, cols]
+            total = hid[rows, cols]
             for lag in range(16):
-                total = total + x[16 - lag:80 - lag, :] * (keep[lag, pl.ds(at, 64), :] * w[lag:lag + 1, :])
-            hid[pl.ds(at, 64), cols] = total
-            return 0
-
-        lax.fori_loop(0, 4, rows, 0)
+                total = total + x[16 - lag:80 - lag, :] * (keep[lag, rows, :] * w[lag:lag + 1, :])
+            hid[rows, cols] = total
 
 
 def wide_w(ref, a, n):
     return jnp.concatenate([ref[2 * n + k, a].reshape(1024, 128) for k in range(2)], axis=1)
 
 
-def feed_forward(gains_ref, w_ref, hid, inner, act, out_ref):
-    rows = hid[...]
+def feed_forward(gains_ref, w_ref, far, hid, inner, act, out_ref):
+    rows = hid[...] + jnp.concatenate([far[s] for s in range(4)], axis=1)
+    hid[...] = rows
     scale = lax.rsqrt(jnp.mean(rows * rows, axis=-1, keepdims=True) + EPS)
     inner[...] = (rows * scale * gains_ref[1:2, :]).astype(BF)
     for n in range(4):
@@ -310,49 +316,114 @@
         out_ref[:, cols] = (hid[:, cols] + dot(act[...], wide_w(w_ref, 2, n))).astype(BF)
 
 
+def pair_run(block, h, e, targets, net):
+    out = [net.copy(block(h), block(h), to) for to in targets]
+    yield
+    yield
+    for one_copy, key in zip(out, (h + e + 4, h - e + 4, h + 2)):
+        one_copy.wait_recv()
+        net.share_cat(block(lax.rem(key, 4)))
+
+
+def all_of_8(block, whole, k, targets, net):
+    out = [net.copy(block(k), block(k), to) for to in targets]
+    yield
+    for one_copy in out:
+        one_copy.wait_recv()
+    net.share(whole)
+
+
+def ring_of_4(block, x, c, up, down, share, net):
+    a = net.copy(block(x), block(x), up)
+    b = net.copy(block(x), block(x), down)
+    yield
+    a.wait_recv()
+    b.wait_recv()
+    key = lax.rem(x + 3 + 2 * c, 4)
+    to = {n: jnp.where(c == 0, up[n], down[n]) for n in up}
+    a = net.copy(block(key), block(key), to)
+    share(block(lax.rem(x + 3, 4)))
+    share(block(lax.rem(x + 1, 4)))
+    yield
+    a.wait_recv()
+    share(block(lax.rem(x + 2, 4)))
+
+
 def flows_of(net, g, catb, wb):
     a = net.at
     x, yl, c, z, yh, zh, y = a["x"], a["yl"], a["c"], a["z"], a["yh"], g["zh"], g["y"]
-    lanes = pl.ds(4 * c, 4)
-
-    def w_y_first(t):
-        lt = 4 * c + t
-        yield from ring_of_8(lambda k: wb.at[lt, :, z, k], y, c, g["y_up"], g["y_down"], net)
-        yield from ring_of_8(lambda k: wb.at[lt, :, k], z, c, g["z_up"], g["z_down"], net)
-
-    def w_z_first(t):
-        lt = 4 * c + t
-        yield from ring_of_8(lambda k: wb.at[lt, :, k, y], z, c, g["z_up"], g["z_down"], net)
-        yield from ring_of_8(lambda k: wb.at[lt, :, :, k], y, c, g["y_up"], g["y_down"], net)
-
-    def cat_x():
-        net.share_cat(catb.at[lanes, x, yl, :, zh])
-        ref = catb.at[lanes, x, yl, :, zh]
+    t_a, t_b, t_c = 4 * c, 4 * c + 1, pl.ds(4 * c + 2, 2)
+
+    def w_a():
+        yield from all_of_8(lambda k: wb.at[t_a, :, z, k], wb.at[t_a, :, z], y, g["ys"], net)
+        yield from ring_of_8(lambda k: wb.at[t_a, :, k], z, c, g["z_up"], g["z_down"], net)
+
+    def w_b():
+        yield from all_of_8(lambda k: wb.at[t_b, :, k, y], wb.at[t_b, :, :, y], z, g["zs"], net)
+        yield from ring_of_8(lambda k: wb.at[t_b, :, :, k], y, c, g["y_up"], g["y_down"], net)
+
+    def quarter(of, zs, ys):
+        rows = pl.ds(pl.multiple_of(8 * (of // 2), 8), 8)
+        return wb.at[4 * c + 2 + lax.rem(of, 2), :, zs, ys, rows]
+
+    def w_c():
+        every = pl.ds(0, 8)
+        yield from all_of_8(lambda k: quarter(x, z, k), quarter(x, z, every), y, g["ys"], net)
+        ring = ring_of_8(lambda k: quarter(x, k, every), z, c, g["z_up"], g["z_down"], net)
+        across = []
+        for keys in ((0,), (7, 1), (6, 2), (5, 3), (4,)):
+            more = next(ring, 0) is None
+            for f in list(across):
+                if next(f, 0) == 0:
+                    across.remove(f)
+            for k in keys:
+                key = lax.rem(z + k, 8)
+                f = ring_of_4(lambda of, key=key: quarter(of, key, every), x, c, g["xs"][0], g["xs"][1], net.share, net)
+                next(f)
+                across.append(f)
+            yield
+        while across:
+            for f in list(across):
+                if next(f, 0) == 0:
+                    across.remove(f)
+            yield
+
+    def swap_y(first, second, both):
+        one_copy = net.copy(first, first, g["y_far"])
+        two = net.copy(second, second, g["y_near"])
+        yield
+        one_copy.wait_recv()
+        two.wait_recv()
+        net.share_cat(both)
+
+    def cat_ab():
+        net.share_cat(catb.at[pl.ds(4 * c, 4), x, yl, :, zh])
+        ref = catb.at[pl.ds(4 * c, 2), x, yl, :, zh]
         out = [net.copy(ref, ref, to) for to in g["xs"]]
         yield
         for one_copy, s in zip(out, (1, 3, 2)):
             one_copy.wait_recv()
-            net.share_cat(catb.at[lanes, lax.rem(x - s + 4, 4), yl, :, zh])
-
-    def swap_y(part):
-        first = net.copy(part(pl.ds(0, 2), yl), part(pl.ds(0, 2), yl), g["y_far"])
-        second = net.copy(part(pl.ds(2, 2), yl), part(pl.ds(2, 2), yl), g["y_near"])
-        yield
-        first.wait_recv()
-        second.wait_recv()
-        net.share_cat(part(pl.ds(0, 4), 1 - yl))
-
-    def cat_y_first():
-        la = pl.ds(4 * c, 2)
-        yield from swap_y(lambda xs, k: catb.at[la, xs, k, :, zh])
-        yield from pair_ring(lambda h: catb.at[la, :, :, :, h], zh, g["e"], 4, g["z_far"], g["z_near"], net)
-
-    def cat_z_first():
-        la = pl.ds(4 * c + 2, 2)
-        yield from pair_ring(lambda h: catb.at[la, :, yl, :, h], zh, g["e"], 4, g["z_far"], g["z_near"], net)
-        yield from swap_y(lambda xs, k: catb.at[la, xs, k])
-
-    return cat_x(), [cat_y_first(), cat_z_first()], [w_y_first(0), w_z_first(2), w_y_first(1), w_z_first(3)]
+            net.share_cat(catb.at[pl.ds(4 * c, 2), lax.rem(x - s + 4, 4), yl, :, zh])
+        both = [cat_a(), cat_b()]
+        while both:
+            tick(both)
+            yield
+
+    def cat_a():
+        yield from swap_y(catb.at[t_a, pl.ds(0, 2), yl, :, zh], catb.at[t_a, pl.ds(2, 2), yl, :, zh],
+                          catb.at[t_a, :, 1 - yl, :, zh])
+        yield from pair_ring(lambda h: catb.at[t_a, :, :, :, h], zh, g["e"], 4, g["z_far"], g["z_near"], net)
+
+    def cat_b():
+        yield from pair_run(lambda h: catb.at[t_b, :, yl, :, h], zh, g["e"], g["z_run"], net)
+        yield from swap_y(catb.at[t_b, pl.ds(0, 2), yl], catb.at[t_b, pl.ds(2, 2), yl], catb.at[t_b, :, 1 - yl])
+
+    def cat_c():
+        yield from pair_run(lambda h: catb.at[t_c, x, yl, :, h], zh, g["e"], g["z_run"], net)
+        yield from swap_y(catb.at[t_c, x, yl, 0], catb.at[t_c, x, yl, 1], catb.at[t_c, x, 1 - yl])
+        yield from ring_of_4(lambda k: catb.at[t_c, k], x, c, g["xs"][0], g["xs"][1], net.share_cat, net)
+
+    return [cat_c(), cat_ab()], [w_a(), w_b(), w_c()]
 
 
 def tick(flows):
@@ -376,9 +447,18 @@
         loads[-1].start()
     fill = []
     mine = pl.ds(pl.multiple_of(16 * yl, 16), 16)
+    part = pl.ds(pl.multiple_of(8 * (x // 2), 8), 8)
+    mine_part = pl.ds(pl.multiple_of(16 * yl + 8 * (x // 2), 8), 8)
+    third = 2 + lax.rem(x, 2)
     for n, ref in enumerate((gate_hbm, up_hbm, down_hbm)):
-        for t in range(8):
-            fill.append(pltpu.make_async_copy(ref.at[mine, 128 * t:128 * t + 128], wb.at[t, n, z, y], fill_sem.at[8 * n + t]))
+        for t in range(3):
+            if t < 2:
+                src = ref.at[mine, pl.ds(pl.multiple_of(512 * c + 128 * t, 128), 128)]
+                dst = wb.at[4 * c + t, n, z, y]
+            else:
+                src = ref.at[mine_part, pl.ds(pl.multiple_of(512 * c + 128 * third, 128), 128)]
+                dst = wb.at[4 * c + third, n, z, y, part]
+            fill.append(pltpu.make_async_copy(src, dst, fill_sem.at[3 * n + t]))
             fill[-1].start()
     near = entry_signals(g)
     loads[2].wait()
@@ -395,7 +475,7 @@
     shared, shared_cat = [], []
     net.share = lambda ref: shared.append(net.copy(ref, ref, g["twin"]))
     net.share_cat = lambda ref: shared_cat.append(net.copy(ref, ref, g["twin"]))
-    cat_x, cats, weights = flows_of(net, g, catb, wb)
+    cats, weights = flows_of(net, g, catb, wb)
     slot = 4 * lax.rem(z, 2) + yh
     group = []
     for to in g["group"]:
@@ -406,47 +486,47 @@
     tick(weights)
     user_tables(base, lens, keep, first, live)
     tap_rows(tl, taps, hr)
-    tap_shifts(hr, ht, 0, 2)
+    tap_shifts(hr, ht, 0, 3)
     for one_copy in group:
         one_copy.wait_recv()
     for k in range(2):
         rows = jnp.concatenate([pairs[k, i].astype(F32) for i in range(8)], axis=0).astype(BF)
         for t in range(4):
             catb[4 * c + t, x, yl, k, zh] = rows[:, 128 * t:128 * t + 128]
-    tick(weights)
-    next(cat_x)
-    tap_shifts(hr, ht, 2, 5)
-    tick([cat_x])
     tick(cats)
     tick(weights)
-    tap_shifts(hr, ht, 7, 5)
+    tap_shifts(hr, ht, 3, 5)
+    tick(cats)
+    tap_shifts(hr, ht, 8, 5)
     tick(cats)
     tick(weights)
-    tap_shifts(hr, ht, 12, 4)
-    tick(cats)
-    tap_flips(ht, h, 0, 8)
+    tap_shifts(hr, ht, 13, 3)
+    tap_flips(ht, h, 0, 4)
     tick(cats)
     tick(weights)
-    tap_flips(ht, h, 8, 8)
+    tap_flips(ht, h, 4, 6)
     tick(cats)
     tick(weights)
+    tap_flips(ht, h, 10, 6)
     while cats:
         tick(cats)
     before.wait_recv()
     for one_copy in shared_cat:
         one_copy.wait_recv()
     look_up(ids, catb, gains, hid, nf, nt)
+    tick(weights)
+    windows(nt, first, ht, 0, 16)
     for s in range(4):
         tick(weights)
-        windows(nt, first, ht, 16 * s, 16)
+        if s < 3:
+            windows(nt, first, ht, 16 * s + 16, 16)
+        near_taps(tl, taps, keep, nf, hid, (2 * s, 2 * s + 1))
         far_taps(ht, h, live, far, s)
-    tick(weights)
-    near_taps(tl, taps, keep, nf, hid, far, range(8))
     while weights:
         tick(weights)
     for one_copy in shared:
         one_copy.wait_recv()
-    feed_forward(gains, wb, hid, inner, act, out_ref)
+    feed_forward(gains, wb, far, hid, inner, act, out_ref)
     net.finish()
 
 
@@ -471,16 +551,16 @@
             pltpu.VMEM((64, 16, 16, 256), BF),
             pltpu.VMEM((64, 256, 256), BF),
             pltpu.VMEM((16, 256, 128), F32),
-            pltpu.VMEM((16, 256), F32),
+            pltpu.VMEM((16, 256), BF),
             pltpu.VMEM((256, 128), F32),
             pltpu.VMEM((256, 1024), F32),
             pltpu.VMEM((272, 1024), F32),
-            pltpu.VMEM((1024, 512), F32),
+            pltpu.VMEM((1024, 512), BF),
             pltpu.VMEM((4, 256, 256), F32),
             pltpu.VMEM((256, 1024), BF),
             pltpu.VMEM((256, 1024), BF),
             pltpu.SemaphoreType.DMA((6,)),
-            pltpu.SemaphoreType.DMA((24,)),
+            pltpu.SemaphoreType.DMA((9,)),
             pltpu.SemaphoreType.DMA((N_SEM,)),
             pltpu.SemaphoreType.DMA((N_SEM,)),
         ],

time: 78.3 us -> 69 us (0.88)
  the two profiles are of different devices: /device:TPU:24 before, /device:TPU:1 now
where the time goes in v3:
time: 69 us; the launch traced here: 68.8 us
  Pallas kernels  66.9 us (97%)
  local copies, waits for them, and re-layouts  1.87 us (3%)
    pallas_call x1, Pallas kernels, body(): pl.pallas_call(layer, out_shape=jax.ShapeDtypeStruct((256, 1024), BF), in...  66.9 us
    unnamed x1, local copies, waits for them, and re-layouts  1.87 us

profile of v3, /device:TPU:1, one launch (start us, length us, event | category | flops | bytes accessed | tf_op | source)
XLA Modules:
  0.0 68.8 jit_solution(6898660620638323499)
XLA Ops:
  0.0 66.9 %shard_map.91 = bf16[256,1024]{1,0:T(8,128)(2,1)} custom-call(s32[32]{0:T(128)} %len_hbm.1, s32[1,256]{1,0:T(1,128)} %bitcast.11, s32[1,1024]{1,0:T(1,128)} %tl_hbm.1, bf16[256,1024]{1,0:T(8,128)(2,1)} %bitcast.6, f32[2,1024]{1,0:T(2,128)} %bitcast.10, bf16[2,1024]{1,0:T(2,128)(2,1)} %cat_hbm.1, bf16[32,1024]{1,0:T(8,128)(2,1)} %bitcast.7, ...), custom_call_target="tpu_custom_call" | custom-call | tf_op jit(solution)/shard_map/pallas_call | solution.py:535
  66.9 1.9 %copy.11 = bf16[256,1024]{1,0:T(8,128)(2,1)} copy(bf16[256,1024]{1,0:T(8,128)(2,1)} %shard_map.91) | data formatting | bytes 1048576

commit v4 on v3

--- a/solution.py
+++ b/solution.py
@@ -423,7 +423,7 @@
         yield from swap_y(catb.at[t_c, x, yl, 0], catb.at[t_c, x, yl, 1], catb.at[t_c, x, 1 - yl])
         yield from ring_of_4(lambda k: catb.at[t_c, k], x, c, g["xs"][0], g["xs"][1], net.share_cat, net)
 
-    return [cat_c(), cat_ab()], [w_a(), w_b(), w_c()]
+    return [cat_c(), cat_ab()], [w_c(), w_a(), w_b()]
 
 
 def tick(flows):

time: 69 us -> 67.9 us (0.984)
  Pallas kernels: 66.9 us -> 65.9 us
    pallas_call x1, Pallas kernels: 66.9 us -> 65.9 us  [body(): pl.pallas_call(layer, out_shape=jax.ShapeDtypeStruct((256, 1024), BF), in...]
where the time goes in v4:
time: 67.9 us; the launch traced here: 67.8 us
  Pallas kernels  65.9 us (97%)
  local copies, waits for them, and re-layouts  1.87 us (3%)
    pallas_call x1, Pallas kernels, body(): pl.pallas_call(layer, out_shape=jax.ShapeDtypeStruct((256, 1024), BF), in...  65.9 us
    unnamed x1, local copies, waits for them, and re-layouts  1.87 us

profile of v4, /device:TPU:1, one launch (start us, length us, event | category | flops | bytes accessed | tf_op | source)
XLA Modules:
  0.0 67.8 jit_solution(12680579199396088961)
XLA Ops:
  0.0 65.9 %shard_map.91 = bf16[256,1024]{1,0:T(8,128)(2,1)} custom-call(s32[32]{0:T(128)} %len_hbm.1, s32[1,256]{1,0:T(1,128)} %bitcast.11, s32[1,1024]{1,0:T(1,128)} %tl_hbm.1, bf16[256,1024]{1,0:T(8,128)(2,1)} %bitcast.6, f32[2,1024]{1,0:T(2,128)} %bitcast.10, bf16[2,1024]{1,0:T(2,128)(2,1)} %cat_hbm.1, bf16[32,1024]{1,0:T(8,128)(2,1)} %bitcast.7, ...), custom_call_target="tpu_custom_call" | custom-call | tf_op jit(solution)/shard_map/pallas_call | solution.py:535
  65.9 1.9 %copy.11 = bf16[256,1024]{1,0:T(8,128)(2,1)} copy(bf16[256,1024]{1,0:T(8,128)(2,1)} %shard_map.91) | data formatting | bytes 1048576
